TPU v7x, 32 devices: a whole 2x2x4 slice. The times are simulated.
32 devices in a mesh: group: 8 (over y, x, core), head: 4 (over z).
Axes of the slice: x: 2, y: 2, z: 4, core: 2. Of those that a mesh axis runs over, the one named last changes fastest.
Arguments:
- hidden_in: bfloat16 [128, 2560], P('group'), may hold values from -6 to 6
- ssm_state: float32 [128, 80, 64, 128], P('group', 'head'), may hold values from -6 to 6
- conv_x_state: bfloat16 [128, 3, 5120], P('group', None, 'head'), may hold values from -6 to 6
- conv_bc_state: bfloat16 [128, 3, 256], P('group'), may hold values from -6 to 6
- token_ids: int32 [128], P('group'), may hold values from 0 to 25599
- ref_logits: bfloat16 [128, 25600], P('group', 'head'), may hold values from -15 to 350
- in_z: bfloat16 [2560, 5120], P('group', 'head'), may hold values from -0.125 to 0.125
- in_x: bfloat16 [2560, 5120], P('group', 'head'), may hold values from -0.125 to 0.125
- in_bc: bfloat16 [2560, 256], P('group'), may hold values from -0.125 to 0.125
- in_dt: bfloat16 [2560, 80], P('group', 'head'), may hold values from -0.125 to 0.125
- out_t: bfloat16 [2560, 5120], P('group', 'head'), may hold values from -0.078125 to 0.078125
- lm_head: bfloat16 [25600, 2560], P('head', 'group'), may hold values from -6 to 6
- conv_wx: float32 [4, 5120], P(None, 'head'), may hold values from -3 to 3
- conv_bx: float32 [5120], P('head'), may hold values from -1.5 to 1.5
- conv_wbc: float32 [4, 256], replicated, may hold values from -3 to 3
- conv_bbc: float32 [256], replicated, may hold values from -1.5 to 1.5
- dt_bias: float32 [80], P('head'), may hold values from -4 to -1
- a_log: float32 [80], P('head'), may hold values from 0 to 2.77
- skip_gain: float32 [80], P('head'), may hold values from 0.5 to 1.5
- norm_in: float32 [2560], replicated, may hold values from 0.5 to 1.5
- norm_gain: float32 [5120], P('head'), may hold values from 0.5 to 1.5
- final_gain: float32 [2560], replicated, may hold values from 0.5 to 1.5
Outputs:
- new_state: float32 [128, 80, 64, 128], P('group', 'head')
- divergence: float32 [128], P('group')
- token_logprob: float32 [128], P('group')
- roll_z: bfloat16 [2560, 5120], P(None, 'head')
- roll_x: bfloat16 [2560, 5120], P(None, 'head')
- roll_bc: bfloat16 [2560, 256], replicated
- roll_dt: bfloat16 [2560, 80], P(None, 'head')
- roll_out: bfloat16 [2560, 5120], P(None, 'head')
All inputs are finite; a program needn't handle non-finite values.
Results may differ from a plain program's by a relative error of at most 0.0102.
Values may be sent and summed in bfloat16 or wider, within the bound.
A program may use at most 128 MiB of HBM per device.

v0:
```python
import functools

import jax
import jax.numpy as jnp
from jax import lax
from jax.experimental import pallas as pl
from jax.experimental.pallas import tpu as pltpu
from jax.sharding import PartitionSpec as P

P_SIZE = 64
EPSILON = 1e-05
MESH = pl.DeviceIdType.MESH


def rms_norm(values, gain):
    return values * lax.rsqrt(jnp.mean(values * values, axis=-1, keepdims=True) + EPSILON) * gain


def causal_conv(history, newest, taps, offset):
    window = jnp.concatenate([history, newest[:, None, :]], axis=1).astype(jnp.float32)
    return jax.nn.silu(jnp.sum(window * taps[None, :, :], axis=1) + offset)


def flip(value, mask):
    bit = 1
    while bit <= mask:
        if mask & bit:
            value = value + bit * (1 - 2 * ((value // bit) % 2))
        bit *= 2
    return value


class Gather:
    def __init__(self, chips, ins, outs, local, send, recv, psend, precv):
        self.chips, self.ins, self.outs = chips, ins, outs
        self.local, self.send, self.recv, self.psend, self.precv = local, send, recv, psend, precv
        group = lax.axis_index("group")
        self.chip, self.core = group // 2, group % 2
        self.pending = []
        self.relay = chips == 4

    def rows(self, a, chip, core, part=None):
        count = self.ins[a].shape[0]
        start = (chip * 2 + core) * count
        if part is not None:
            count = count // 2
            start = start + part * count
        return pl.ds(pl.multiple_of(start, 16), count)

    def copy(self, src, dst, chip, core, ssem, rsem):
        made = pltpu.make_async_remote_copy(
            src_ref=src, dst_ref=dst, send_sem=ssem, recv_sem=rsem,
            device_id={"group": chip * 2 + core}, device_id_type=MESH,
        )
        made.start()
        self.pending.append(made)
        return made

    def start(self, a):
        src = self.ins[a]
        own = self.outs[a].at[self.rows(a, self.chip, self.core)]
        loc = pltpu.make_async_copy(src, own, self.local.at[a])
        loc.start()
        self.far = getattr(self, "far", {})
        peers = [1, 2] if self.relay else range(1, self.chips)
        for m in peers:
            self.far[a, m] = self.copy(
                src, own, flip(self.chip, m), self.core, self.send.at[a, m], self.recv.at[a, m])
        self.near = getattr(self, "near", {})
        self.near[a, 0] = self.copy(
            src, own, self.chip, 1 - self.core, self.psend.at[a, 0], self.precv.at[a, 0])
        self.locals = getattr(self, "locals", {})
        self.locals[a] = loc

    def hand_on(self, a, m, chip, part, slot):
        view = self.outs[a].at[self.rows(a, chip, self.core, part)]
        self.near[a, slot] = self.copy(
            view, view, self.chip, 1 - self.core, self.psend.at[a, slot], self.precv.at[a, slot])

    def relay_near(self, a):
        if self.relay:
            for m, part in ((1, 0), (2, 1)):
                self.far[a, m].wait_recv()
                source = flip(self.chip, m)
                view = self.outs[a].at[self.rows(a, source, self.core, part)]
                self.far[a, 3 + part] = self.copy(
                    view, view, flip(self.chip, 3 - m), self.core,
                    self.send.at[a, 3 + part], self.recv.at[a, 3 + part])
                self.hand_on(a, m, source, None, m)
        else:
            for m in range(1, self.chips):
                self.far[a, m].wait_recv()
                self.hand_on(a, m, flip(self.chip, m), None, m)

    def relay_far(self, a):
        if self.relay:
            for part in (0, 1):
                self.far[a, 3 + part].wait_recv()
                self.hand_on(a, 3, flip(self.chip, 3), part, 3 + part)

    def arrive(self, a):
        for (b, _), made in self.near.items():
            if b == a:
                made.wait_recv()
        self.locals[a].wait()

    def drain(self):
        for made in self.pending:
            made.wait_send()


def gather_sems(count, chips):
    slots = max(chips, 5)
    dma = pltpu.SemaphoreType.DMA
    return [dma((count,)), dma((count, slots)), dma((count, slots)), dma((count, slots)), dma((count, slots))]


def greet(groups, heads):
    barrier = pltpu.get_barrier_semaphore()
    group, head = lax.axis_index("group"), lax.axis_index("head")
    for j in range(1, groups):
        pl.semaphore_signal(barrier, inc=1, device_id={"group": (group + j) % groups}, device_id_type=MESH)
    for j in range(1, heads):
        pl.semaphore_signal(barrier, inc=1, device_id={"head": (head + j) % heads}, device_id_type=MESH)
    pl.semaphore_wait(barrier, groups - 1 + heads - 1)


def gather_kernel(groups, count, *refs):
    ins, outs, sems = refs[:count], refs[count:2 * count], refs[2 * count:]
    work = Gather(groups // 2, ins, outs, *sems)
    greet(groups, 1)
    for a in range(count):
        work.start(a)
    for a in range(count):
        work.relay_near(a)
        if a:
            work.relay_far(a - 1)
    work.relay_far(count - 1)
    for a in range(count):
        work.arrive(a)
    work.drain()


def gather(groups, arrays):
    count = len(arrays)
    any_spec = pl.BlockSpec(memory_space=pl.ANY)
    return pl.pallas_call(
        functools.partial(gather_kernel, groups, count),
        out_shape=[jax.ShapeDtypeStruct((groups * v.shape[0], v.shape[1]), v.dtype) for v in arrays],
        in_specs=[any_spec] * count,
        out_specs=[any_spec] * count,
        scratch_shapes=gather_sems(count, groups // 2),
        compiler_params=pltpu.CompilerParams(collective_id=0, has_side_effects=True),
        name="gather_in",
    )(*arrays)


def project_kernel(steps, normed_ref, *refs):
    count = len(refs) // 4
    weights, sums, copies, totals = (refs[n * count:(n + 1) * count] for n in range(4))
    step = pl.program_id(0)

    @pl.when(step == 0)
    def _():
        for total in totals:
            total[...] = jnp.zeros_like(total)

    for weight, copied, total in zip(weights, copies, totals):
        block = weight[...]
        copied[...] = block
        total[...] += jnp.dot(normed_ref[...], block, preferred_element_type=jnp.float32)

    @pl.when(step == steps - 1)
    def _():
        for out, total in zip(sums, totals):
            out[...] = total[...].astype(out.dtype)


def project(normed, weights):
    seqs, depth = normed.shape
    steps = 5
    rows = depth // steps
    whole = lambda w: pl.BlockSpec((seqs, w.shape[1]), lambda k: (0, 0))
    block = lambda w: pl.BlockSpec((rows, w.shape[1]), lambda k: (k, 0))
    made = pl.pallas_call(
        functools.partial(project_kernel, steps),
        grid=(steps,),
        in_specs=[pl.BlockSpec((seqs, rows), lambda k: (0, k))] + [block(w) for w in weights],
        out_specs=[whole(w) for w in weights] + [block(w) for w in weights],
        out_shape=[jax.ShapeDtypeStruct((seqs, w.shape[1]), jnp.bfloat16) for w in weights]
        + [jax.ShapeDtypeStruct(w.shape, w.dtype) for w in weights],
        scratch_shapes=[pltpu.VMEM((seqs, w.shape[1]), jnp.float32) for w in weights],
        name="project",
    )(normed, *weights)
    return made[:len(weights)], made[len(weights):]


def state_kernel(each, decay_ref, inflow_ref, b_ref, c_ref, state_ref, new_ref, y_ref):
    heads, width, size = state_ref.shape[1:]

    def pair(row):
        high = row.astype(jnp.bfloat16).astype(jnp.float32)
        return high, row - high

    for n in range(each):
        seq = pl.program_id(0) * each + n
        high, low = pair(inflow_ref[n])
        b_high, b_low = pair(b_ref[n])
        place = lax.broadcasted_iota(jnp.int32, (16, heads * width), 0)
        left = jnp.where(place < 2, high, jnp.where(place < 4, low, 0.0)).astype(jnp.bfloat16)
        place = lax.broadcasted_iota(jnp.int32, (16, size), 0)
        right = jnp.where(place % 2 == 0, b_high, b_low).astype(jnp.bfloat16)
        inflow = lax.dot_general(
            left, right, (((0,), (0,)), ((), ())), preferred_element_type=jnp.float32)
        for h in range(heads):
            new_ref[n, h] = decay_ref[seq, h] * state_ref[n, h] + inflow[h * width:(h + 1) * width]
        new = new_ref[n].reshape(heads * width, size).astype(jnp.bfloat16)
        c = jnp.broadcast_to(c_ref[n], (16, size)).astype(jnp.bfloat16)
        y = lax.dot_general(c, new, (((1,), (1,)), ((), ())), preferred_element_type=jnp.float32)
        y_ref[n] = y[0:1]


def state_step(decay, inflow, b_vals, c_vals, state):
    seqs, heads, width, size = state.shape
    each = 2
    row = lambda wide: pl.BlockSpec((each, 1, wide), lambda s: (s, 0, 0))
    block = pl.BlockSpec((each, heads, width, size), lambda s: (s, 0, 0, 0))
    new, y = pl.pallas_call(
        functools.partial(state_kernel, each),
        grid=(seqs // each,),
        in_specs=[pl.BlockSpec(memory_space=pltpu.SMEM), row(heads * width), row(size), row(size), block],
        out_specs=[block, row(heads * width)],
        out_shape=[jax.ShapeDtypeStruct(state.shape, jnp.float32),
                   jax.ShapeDtypeStruct((seqs, 1, heads * width), jnp.float32)],
        name="state_step",
    )(decay, inflow[:, None], b_vals[:, None], c_vals[:, None], state)
    return new, y[:, 0]


def halves(column, lanes, first, split):
    high = column.astype(jnp.bfloat16).astype(jnp.float32)
    return jnp.where(lanes < split, high, column - high)


def tail_kernel(
    groups, heads, seqs,
    gated_ref, hid_ref, ngain_ref, fgain_ref, out_t_ref, lm_ref, refl_ref, token_ref, out_hbm,
    roll_out, result_ref,
    gall, hall, mix, pairs, pair_in, sums, sums_in, square, square_in, squares_out, squares_in, stat,
    gsend, grecv, hsend, hrecv, msend, mrecv, psend, precv, ssend, srecv, tsend, trecv,
    *gsems,
):
    chips = groups // 2
    group, head = lax.axis_index("group"), lax.axis_index("head")
    chip, core = group // 2, group % 2
    wide = mix.shape[2]
    depth = out_t_ref.shape[0]
    vocab = lm_ref.shape[1]
    parts = pairs.shape[0]
    width = vocab // parts
    rows = groups * seqs
    pending = []

    def send(src, dst, device, ssem, rsem):
        made = pltpu.make_async_remote_copy(
            src_ref=src, dst_ref=dst, send_sem=ssem, recv_sem=rsem, device_id=device, device_id_type=MESH)
        made.start()
        pending.append(made)
        return made

    work = Gather(chips, [out_hbm], [roll_out], *gsems)
    greet(groups, heads)
    first = []
    for j in range(1, groups):
        peer = (group + j) % groups
        first.append(send(gated_ref, gall.at[group], {"group": peer}, gsend.at[j], grecv.at[j]))
        first.append(send(hid_ref.at[peer], hall.at[group], {"group": peer}, hsend.at[j], hrecv.at[j]))
    work.start(0)
    gall[group] = gated_ref[...]
    hall[group] = hid_ref[group]
    for made in first:
        made.wait_recv()

    gated = gall[...].reshape(rows, gall.shape[2]).astype(jnp.float32)
    squares = jnp.sum(gated * gated, axis=-1, keepdims=True)
    scaled = (gated * ngain_ref[...]).astype(jnp.bfloat16)
    out_rows = out_t_ref[...]
    if wide > depth:
        out_rows = jnp.concatenate(
            [out_rows, jnp.zeros((wide - depth, out_rows.shape[1]), jnp.bfloat16)], axis=0)
    partial = lax.dot_general(
        scaled, out_rows, (((1,), (1,)), ((), ())), preferred_element_type=jnp.float32)
    lanes = lax.broadcasted_iota(jnp.int32, (rows, wide), 1)
    middle = (depth + wide) // 2
    mix[0] = jnp.where(lanes < depth, partial, halves(squares, lanes, depth, middle)).astype(jnp.bfloat16)
    mixes = [
        send(mix.at[0], mix.at[j], {"head": (head + j) % heads}, msend.at[j], mrecv.at[j])
        for j in range(1, heads)
    ]
    for made in mixes:
        made.wait_recv()
    work.relay_near(0)
    total = jnp.sum(mix[...].astype(jnp.float32), axis=0)
    square_total = total[:, depth:depth + 1] + total[:, middle:middle + 1]
    inner = gall.shape[2] * heads
    hidden = hall[...].reshape(rows, wide).astype(jnp.float32)
    stream = hidden + total * lax.rsqrt(square_total / inner + EPSILON)
    stream = jnp.where(lanes < depth, stream, 0.0)
    final_squares = jnp.sum(stream * stream, axis=-1, keepdims=True)
    final = (stream * fgain_ref[...]).astype(jnp.bfloat16)

    def by_core(values):
        parts = values.reshape(chips, 2, seqs, values.shape[1])
        return jnp.concatenate(
            [parts[:, 0].reshape(chips * seqs, -1), parts[:, 1].reshape(chips * seqs, -1)], axis=0)

    final = by_core(final.astype(jnp.float32)).astype(jnp.bfloat16)[:, :depth]
    final_squares = by_core(jnp.broadcast_to(final_squares, (rows, 128)))
    tail_lanes = lax.broadcasted_iota(jnp.int32, (rows, 128), 1)
    packed = halves(final_squares, tail_lanes, 0, 64).astype(jnp.bfloat16)
    half = chips * seqs
    other = {"group": chip * 2 + 1 - core}
    square[0], square[1] = packed[:half], packed[half:]
    pair_sends = [send(square.at[1 - core], square_in, other, psend.at[parts], precv.at[parts])]
    last = []

    def out(source, target, t):
        for m in range(1, chips):
            peer = flip(chip, m)
            last.append(send(
                source.at[peer], target.at[m], {"group": peer * 2 + core}, ssend.at[t, m], srecv.at[t, m]))
        target[0] = source[chip]

    def join(t):
        pair_sends[t + 1].wait_recv()
        joined = pairs[t, core].astype(jnp.float32) + pair_in[t].astype(jnp.float32)
        sums[t] = joined.astype(jnp.bfloat16).reshape(chips, seqs, width)
        out(sums.at[t], sums_in.at[t], t)

    for t in range(parts):
        block = lax.dot_general(
            final, lm_ref[:, t * width:(t + 1) * width], (((1,), (0,)), ((), ())),
            preferred_element_type=jnp.float32).astype(jnp.bfloat16)
        pairs[t, 0], pairs[t, 1] = block[:half], block[half:]
        pair_sends.append(send(pairs.at[t, 1 - core], pair_in.at[t], other, psend.at[t], precv.at[t]))
        if t == 0:
            pair_sends[0].wait_recv()
            rest = square[core].astype(jnp.float32) + square_in[...].astype(jnp.float32)
            rest = rest[:, 0:1] + rest[:, 64:65]
            split = halves(rest, lax.broadcasted_iota(jnp.int32, (half, 128), 1), 0, 64)
            squares_out[...] = split.astype(jnp.bfloat16).reshape(chips, seqs, 128)
            out(squares_out, squares_in, parts)
        else:
            join(t - 1)
    join(parts - 1)
    work.relay_far(0)
    for made in last:
        made.wait_recv()

    square_sum = jnp.sum(squares_in[...].astype(jnp.float32), axis=0)
    mean_square = (square_sum[:, 0:1] + square_sum[:, 64:65]) / (depth * groups)
    logits = jnp.concatenate(
        [jnp.sum(sums_in[t].astype(jnp.float32), axis=0) for t in range(parts)], axis=1)
    logits = logits * lax.rsqrt(mean_square + EPSILON)
    reference = refl_ref[...].astype(jnp.float32)
    columns = lax.broadcasted_iota(jnp.int32, (seqs, vocab), 1) + head * vocab
    picked = jnp.sum(jnp.where(columns == token_ref[...], logits, 0.0), axis=-1, keepdims=True)
    top = jnp.max(logits, axis=-1, keepdims=True)
    ref_top = jnp.max(reference, axis=-1, keepdims=True)
    weights = jnp.exp(reference - ref_top)
    values = (
        top,
        jnp.sum(jnp.exp(logits - top), axis=-1, keepdims=True),
        ref_top,
        jnp.sum(weights, axis=-1, keepdims=True),
        jnp.sum(weights * (reference - logits), axis=-1, keepdims=True),
        picked,
    )
    slot = lax.broadcasted_iota(jnp.int32, (seqs, 128), 1)
    mine = jnp.zeros((seqs, 128), jnp.float32)
    for n, value in enumerate(values):
        mine = jnp.where(slot == n, value, mine)
    stat[0] = mine
    stats = [
        send(stat.at[0], stat.at[j], {"head": (head + j) % heads}, tsend.at[j], trecv.at[j])
        for j in range(1, heads)
    ]
    for made in stats:
        made.wait_recv()
    every = stat[...]
    pick = lambda n: every[:, :, n:n + 1]
    top = jnp.max(pick(0), axis=0)
    ref_top = jnp.max(pick(2), axis=0)
    factor = jnp.exp(pick(0) - top[None])
    ref_factor = jnp.exp(pick(2) - ref_top[None])
    roll_sum = jnp.sum(pick(1) * factor, axis=0)
    ref_sum = jnp.sum(pick(3) * ref_factor, axis=0)
    cross = jnp.sum(pick(4) * ref_factor, axis=0)
    picked = jnp.sum(pick(5), axis=0)
    lse_roll = top + jnp.log(roll_sum)
    lse_ref = ref_top + jnp.log(ref_sum)
    result_ref[...] = jnp.where(slot == 0, cross / ref_sum - lse_ref + lse_roll, picked - lse_roll)

    work.arrive(0)
    work.drain()
    for made in pending:
        made.wait_send()


def tail(groups, heads, gated, hid, ngain, fgain, out_t, lm_head, ref_logits, tokens):
    seqs, inner = gated.shape
    depth = out_t.shape[0]
    wide = hid.shape[2]
    vocab = lm_head.shape[1]
    parts = 5
    width = vocab // parts
    chips = groups // 2
    vmem, any_spec = pl.BlockSpec(memory_space=pltpu.VMEM), pl.BlockSpec(memory_space=pl.ANY)
    dma = pltpu.SemaphoreType.DMA
    bf16 = jnp.bfloat16
    return pl.pallas_call(
        functools.partial(tail_kernel, groups, heads, seqs),
        out_shape=[jax.ShapeDtypeStruct((groups * depth, inner), bf16),
                   jax.ShapeDtypeStruct((seqs, 128), jnp.float32)],
        in_specs=[vmem] * 8 + [any_spec],
        out_specs=[any_spec, vmem],
        scratch_shapes=[
            pltpu.VMEM((groups, seqs, inner), bf16),
            pltpu.VMEM((groups, seqs, wide), bf16),
            pltpu.VMEM((heads, groups * seqs, wide), bf16),
            pltpu.VMEM((parts, 2, chips * seqs, width), bf16),
            pltpu.VMEM((parts, chips * seqs, width), bf16),
            pltpu.VMEM((parts, chips, seqs, width), bf16),
            pltpu.VMEM((parts, chips, seqs, width), bf16),
            pltpu.VMEM((2, chips * seqs, 128), bf16),
            pltpu.VMEM((chips * seqs, 128), bf16),
            pltpu.VMEM((chips, seqs, 128), bf16),
            pltpu.VMEM((chips, seqs, 128), bf16),
            pltpu.VMEM((heads, seqs, 128), jnp.float32),
            dma((groups,)), dma((groups,)), dma((groups,)), dma((groups,)),
            dma((heads,)), dma((heads,)), dma((parts + 1,)), dma((parts + 1,)),
            dma((parts + 1, chips)), dma((parts + 1, chips)), dma((heads,)), dma((heads,)),
        ] + gather_sems(1, chips),
        compiler_params=pltpu.CompilerParams(
            collective_id=1, has_side_effects=True, vmem_limit_bytes=56 * 1024 * 1024),
        name="tail",
    )(gated, hid, ngain, fgain, out_t, lm_head, ref_logits, tokens, out_t)


def shards(
    groups, heads,
    hidden_in, ssm_state, conv_x_state, conv_bc_state, token_ids, ref_logits,
    in_z, in_x, in_bc, in_dt, out_t, lm_head,
    conv_wx, conv_bx, conv_wbc, conv_bbc, dt_bias, a_log, skip_gain, norm_in, norm_gain, final_gain,
):
    local_heads = a_log.shape[0]
    dt_wide = jnp.pad(in_dt, ((0, 0), (0, -in_dt.shape[1] % 128)))
    roll_bc, dt_all, roll_x, roll_z = gather(groups, [in_bc, dt_wide, in_x, in_z])
    stream_in = hidden_in.astype(jnp.float32)
    normed = rms_norm(stream_in, norm_in).astype(jnp.bfloat16)
    (gate_branch, x_branch, bc_branch, step_raw), (roll_z, roll_x, roll_bc, dt_all) = project(
        normed, (roll_z, roll_x, roll_bc, dt_all))
    roll_dt = dt_all[:, :local_heads]
    step_raw = step_raw[:, :local_heads]
    x_conv = causal_conv(conv_x_state, x_branch, conv_wx, conv_bx)
    bc_conv = causal_conv(conv_bc_state, bc_branch, conv_wbc, conv_bbc)
    state_size = bc_conv.shape[1] // 2
    b_vals = bc_conv[:, :state_size]
    c_vals = bc_conv[:, state_size:]
    step = jax.nn.softplus(step_raw.astype(jnp.float32) + dt_bias)
    decay = jnp.exp(-step * jnp.exp(a_log))
    seqs = x_conv.shape[0]
    spread = lambda v: jnp.repeat(v, P_SIZE, axis=-1)
    new_state, ssm_out = state_step(
        decay, spread(step) * x_conv, b_vals, c_vals, ssm_state)
    ssm_out = ssm_out + spread(skip_gain)[None] * x_conv
    gated = (ssm_out * jax.nn.silu(gate_branch.astype(jnp.float32))).astype(jnp.bfloat16)
    depth = out_t.shape[0]
    extra = -depth % 128 or 128
    hid = hidden_in.reshape(seqs, groups, depth).transpose(1, 0, 2)
    hid = jnp.pad(hid, ((0, 0), (0, 0), (0, extra)))
    fgain = lax.dynamic_slice(final_gain, (lax.axis_index("group") * depth,), (depth,))
    fgain = jnp.pad(fgain, (0, extra))[None]
    roll_out, result = tail(
        groups, heads, gated, hid, norm_gain[None], fgain, out_t, lm_head.T, ref_logits, token_ids[:, None])
    return (new_state, result[:, 0], result[:, 1], roll_z, roll_x, roll_bc, roll_dt, roll_out)


def solution(mesh):
    return jax.shard_map(
        functools.partial(shards, mesh.shape["group"], mesh.shape["head"]),
        mesh=mesh,
        in_specs=(
            P("group", None),
            P("group", "head", None, None),
            P("group", None, "head"),
            P("group", None, None),
            P("group"),
            P("group", "head"),
            P("group", "head"),
            P("group", "head"),
            P("group", None),
            P("group", "head"),
            P("group", "head"),
            P("head", "group"),
            P(None, "head"),
            P("head"),
            P(),
            P(),
            P("head"),
            P("head"),
            P("head"),
            P(),
            P("head"),
            P(),
        ),
        out_specs=(
            P("group", "head", None, None),
            P("group"),
            P("group"),
            P(None, "head"),
            P(None, "head"),
            P(),
            P(None, "head"),
            P(None, "head"),
        ),
        check_vma=False,
    )
```

profile of v0, /device:TPU:1, one launch (start us, length us, event | category | flops | bytes accessed | tf_op | source)
XLA Modules:
  0.0 177.0 jit_solution(5700333840193086981)
XLA Ops:
  0.6 0.7 exp.31
  1.3 1.0 fusion
  2.3 0.8 dynamic_slice.3
  3.7 1.3 broadcast_in_dim.42.ngain_ref
  5.0 1.3 copy.39.token_ref
  6.3 0.7 broadcast_in_dim.41
  7.1 1.6 fusion.2.normed_ref
  8.7 0.9 copy.35
  9.6 0.7 pad.12.refs_1_
  10.2 1.0 reshape.88
  11.3 0.7 pad.13.hid_ref
  11.9 70.6 %gather_in.1 = (bf16[2560,256]{1,0:T(8,128)(2,1)}, bf16[2560,128]{1,0:T(8,128)(2,1)}, bf16[2560,1280]{1,0:T(8,128)(2,1)}, bf16[2560,1280]{1,0:T(8,128)(2,1)}) custom-call(bf16[320,256]{1,0:T(8,128)(2,1)} %refs_0_.1, bf16[320,128]{1,0:T(8,128)(2,1)} %pad.12.refs_1_, bf16[320,1280]{1,0:T(8,128)(2,1)} %refs_2_.1, bf16[320,1280]{1,0:T(8,128)(2,1)} %refs_3_.1), custom_call_target="tpu_custom_call" | custom-call | tf_op jit(solution)/shard_map/gather_in/pallas_call | solution.py:147
  82.7 13.3 %project.1 = (bf16[16,1280]{1,0:T(8,128)(2,1)}, bf16[16,1280]{1,0:T(8,128)(2,1)}, bf16[16,256]{1,0:T(8,128)(2,1)}, bf16[16,128]{1,0:T(8,128)(2,1)}, bf16[2560,12...) custom-call(bf16[16,2560]{1,0:T(8,128)(2,1)} %fusion.2.normed_ref, ...), custom_call_target="tpu_custom_call" | custom-call | tf_op jit(solution)/shard_map/project/pallas_call | solution.py:185
  96.0 1.3 compare_select_fusion
  97.3 0.7 multiply_reduce_fusion.1
  98.1 0.6 fusion.8
  98.7 0.8 multiply_reduce_fusion
  99.5 2.0 %copy.40 = bf16[2560,20]{0,1:T(8,128)(2,1)} copy(bf16[2560,20]{1,0:T(8,128)(2,1)} %bitcast.23) | data formatting | bytes 204800
  101.8 0.7 copy.36.inflow_ref
  102.5 12.2 %state_step.1 = (f32[16,20,64,128]{3,2,1,0:T(8,128)}, f32[16,1,1280]{2,1,0:T(1,128)}) custom-call(f32[16,20]{1,0:T(8,128)} %get-tuple-element.61.decay_ref, f32[16,1,1280]{2,1,0:T(1,128)} %copy.36.inflow_ref, f32[16,1,128]{2,1,0:T(1,128)} %bitcast.27, f32[16,1,128]{2,1,0:T(1,128)} %bitcast.26, f32[16,20,64,128]{3,2,1,0:T(8,128)} %state_ref.1), custom_call_target="tpu_custom_call" | custom-call | tf_op jit(solution)/shard_map/state_step/pallas_call | solution.py:228
  114.7 1.6 fusion.7.gated_ref
  116.2 53.2 %tail.1 = (bf16[2560,1280]{1,0:T(8,128)(2,1)}, f32[16,128]{1,0:T(8,128)}) custom-call(bf16[16,1280]{1,0:T(8,128)(2,1)} %fusion.7.gated_ref, bf16[8,16,384]{2,1,0:T(8,128)(2,1)} %pad.13.hid_ref, f32[1,1280]{1,0:T(1,128)} %broadcast_in_dim.42.ngain_ref, f32[1,384]{1,0:T(1,128)} %broadcast_in_dim.43.fgain_ref, bf16[320,1280]{1,0:T(8,128)(2,1)} %out_hbm.1, ...), custom_call_target="tpu_custom_call" | custom-call | tf_op jit(solution)/shard_map/tail/pallas_call | solution.py:421
  169.4 1.5 slice_reduce_fusion
  170.9 6.1 %copy.48 = bf16[2560,1280]{1,0:T(8,128)(2,1)} copy(bf16[2560,1280]{1,0:T(8,128)(2,1)} %get-tuple-element.77) | data formatting | bytes 13107200
  (25 shorter events, 1.0 us)
Async XLA Ops:
  82.6 13.4 %copy-start.7 = (f32[20]{0:T(128)S(1)}, f32[20]{0:T(128)}, u32[]{:S(2)}) copy-start(f32[20]{0:T(128)} %param.38) | copy-start | bytes 244
  82.6 14.7 %copy-start.3 = (bf16[16,3,256]{2,0,1:T(8,128)(2,1)S(1)}, bf16[16,3,256]{2,0,1:T(8,128)(2,1)}, u32[]{:S(2)}) copy-start(bf16[16,3,256]{2,0,1:T(8,128)(2,1)} %param.25) | copy-start | bytes 73732
  82.6 14.7 %copy-start.5 = (f32[4,256]{1,0:T(4,128)S(1)}, f32[4,256]{1,0:T(4,128)}, u32[]{:S(2)}) copy-start(f32[4,256]{1,0:T(4,128)} %param.36) | copy-start | bytes 12292
  82.6 15.4 %copy-start.6 = (f32[256]{0:T(256)S(1)}, f32[256]{0:T(256)}, u32[]{:S(2)}) copy-start(f32[256]{0:T(256)} %param.37) | copy-start | bytes 3076
  82.7 16.0 %copy-start = (bf16[16,3,1280]{2,0,1:T(8,128)(2,1)S(1)}, bf16[16,3,1280]{2,0,1:T(8,128)(2,1)}, u32[]{:S(2)}) copy-start(bf16[16,3,1280]{2,0,1:T(8,128)(2,1)} %param.24) | copy-start | bytes 368644
  82.7 16.0 %copy-start.4 = (f32[4,1280]{1,0:T(4,128)S(1)}, f32[4,1280]{1,0:T(4,128)}, u32[]{:S(2)}) copy-start(f32[4,1280]{1,0:T(4,128)} %param.34) | copy-start | bytes 61444
  82.7 19.0 %copy-start.2 = (f32[1280]{0:T(1024)S(1)}, f32[1280]{0:T(1024)}, u32[]{:S(2)}) copy-start(f32[1280]{0:T(1024)} %param.35) | copy-start | bytes 15364
  96.0 18.7 %copy-start.1 = (bf16[16,1280]{1,0:T(8,128)(2,1)S(1)}, bf16[16,1280]{1,0:T(8,128)(2,1)}, u32[]{:S(2)}) copy-start(bf16[16,1280]{1,0:T(8,128)(2,1)} %get-tuple-element.33) | copy-start | bytes 122884
where the time goes:
time: 180 us; the launch traced here: 177 us
  Pallas kernels  149 us (83%)
  local copies, waits for them, and re-layouts  19.8 us (11%)
  other arithmetic  7.09 us (4%)
    pallas_call x1, Pallas kernels, gather(): pl.pallas_call(functools.partial(gather_kernel, groups, count), out_shape...  70.6 us
    pallas_call x1, Pallas kernels, tail(): pl.pallas_call(functools.partial(tail_kernel, groups, heads, seqs), out_s...  53.2 us
    pallas_call x1, Pallas kernels, project(): pl.pallas_call(functools.partial(project_kernel, steps), grid=(steps,), i...  13.3 us
    pallas_call x1, Pallas kernels, state_step(): pl.pallas_call(functools.partial(state_kernel, each), grid=(seqs // each,...  12.2 us
    unnamed x19, local copies, waits for them, and re-layouts  8.98 us

commit v1 on v0

v1 whole, which is shorter than its diff:
```python
import functools

import jax
import jax.numpy as jnp
from jax import lax
from jax.experimental import pallas as pl
from jax.experimental.pallas import tpu as pltpu
from jax.sharding import PartitionSpec as P

P_SIZE = 64
EPSILON = 1e-05
AHEAD = 2
PIECES = 5
PARTS = 5
MESH = pl.DeviceIdType.MESH


def flip(value, mask):
    bit = 1
    while bit <= mask:
        if mask & bit:
            value = value + bit * (1 - 2 * ((value // bit) % 2))
        bit *= 2
    return value


def greet(groups, heads):
    barrier = pltpu.get_barrier_semaphore()
    group, head = lax.axis_index("group"), lax.axis_index("head")
    for j in range(1, groups):
        pl.semaphore_signal(barrier, inc=1, device_id={"group": (group + j) % groups}, device_id_type=MESH)
    for j in range(1, heads):
        pl.semaphore_signal(barrier, inc=1, device_id={"head": (head + j) % heads}, device_id_type=MESH)
    pl.semaphore_wait(barrier, groups - 1 + heads - 1)


class Links:
    def __init__(self):
        self.pending = []

    def send(self, src, dst, device, ssem, rsem):
        made = pltpu.make_async_remote_copy(
            src_ref=src, dst_ref=dst, send_sem=ssem, recv_sem=rsem, device_id=device, device_id_type=MESH)
        made.start()
        self.pending.append(made)
        return made

    def drain(self):
        for made in self.pending:
            made.wait_send()


class Bulk:
    def __init__(self, links, chips, units, send, recv, psend, precv):
        self.links, self.chips, self.units = links, chips, units
        self.sems, self.pair_sems = (send, recv), (psend, precv)
        group = lax.axis_index("group")
        self.chip, self.core = group // 2, group % 2
        self.relay = chips == 4
        self.far, self.near = {}, []
        self.next = 0
        for k in range(AHEAD):
            self.own(k)

    def rows(self, k, chip):
        src, _, first, count = self.units[k]
        start = (chip * 2 + self.core) * src.shape[0] + first
        return self.units[k][1].at[pl.ds(pl.multiple_of(start, 16), count)]

    def across(self, k, m, src, dst, slot):
        send, recv = self.sems
        device = {"group": flip(self.chip, m) * 2 + self.core}
        self.far[k, slot] = self.links.send(src, dst, device, send.at[k, slot], recv.at[k, slot])

    def hand(self, k, src, dst, slot):
        send, recv = self.pair_sems
        device = {"group": self.chip * 2 + 1 - self.core}
        self.near.append(self.links.send(src, dst, device, send.at[k, slot], recv.at[k, slot]))

    def own(self, k):
        src, _, first, count = self.units[k]
        src, dst = src.at[pl.ds(first, count)], self.rows(k, self.chip)
        for m in [1, 2] if self.relay else range(1, self.chips):
            self.across(k, m, src, dst, m)
        self.hand(k, src, dst, 0)

    def step(self):
        k = self.next
        self.next += 1
        order = range(1, self.chips)
        if self.relay:
            order = (1, 2) if k % 2 == 0 else (2, 1)
        for m in order:
            self.far[k, m].wait_recv()
            view = self.rows(k, flip(self.chip, m))
            if self.relay and m == order[0]:
                self.across(k, 3 - m, view, view, 3)
            self.hand(k, view, view, m)
        if k + AHEAD < len(self.units):
            self.own(k + AHEAD)
        if k:
            self.last(k - 1)

    def last(self, k):
        if self.relay:
            self.far[k, 3].wait_recv()
            view = self.rows(k, flip(self.chip, 3))
            self.hand(k, view, view, 3)

    def pump(self, count):
        for _ in range(count):
            if self.next < len(self.units):
                self.step()

    def finish(self):
        self.pump(len(self.units))
        self.last(len(self.units) - 1)
        for made in self.near:
            made.wait_recv()


def halves(column, lanes, first, split):
    high = column.astype(jnp.bfloat16).astype(jnp.float32)
    return jnp.where(lanes < split, high, column - high)


def rms_scale(mean_square):
    return lax.rsqrt(mean_square + EPSILON)


def silu(values):
    return values * jax.nn.sigmoid(values)


def window(values, first, width):
    wide = width + (-width % 128 or 128)
    span = wide + 128
    start = min(first // 128 * 128, values.shape[1] - span)
    return pltpu.roll(values[:, start:start + span], (start - first) % span, 1)[:, :wide]


def own_window(values, group, groups, width):
    chosen = window(values, 0, width)
    for p in range(1, groups):
        chosen = jnp.where(group == p, window(values, p * width, width), chosen)
    return chosen


def step_kernel(
    groups, heads, local_heads,
    hid_ref, cx_ref, cbc_ref, token_ref, refl_ref, dt_ref, small_ref,
    wx_ref, bx_ref, wbc_ref, bbc_ref, norm_in_ref, ngain_ref, fgain_ref,
    state_hbm, z_hbm, x_hbm, bc_hbm, out_hbm, lm_hbm,
    new_ref, z_all, x_all, bc_all, out_all, dt_all, result_ref,
    lm_ref, hsend, hall, ppairs, ppair_in, psum, psum_in, dt_pad, inflow_ref, b_ref, c_ref, decay_ref, y_ref,
    gall, mix, pairs, pair_in, sums, sums_in, square, square_in, squares_out, squares_in, stat,
    load, bsend, brecv, bpsend, bprecv, hsem, hrsem, dsem, drsem, qsem, qrsem, rsem, rrsem, gsem, grsem,
    msend, mrecv, psend, precv, ssend, srecv, tsend, trecv,
):
    f32, bf16 = jnp.float32, jnp.bfloat16
    chips = groups // 2
    group, head = lax.axis_index("group"), lax.axis_index("head")
    chip, core = group // 2, group % 2
    seqs, model = hid_ref.shape
    depth, inner = z_hbm.shape
    wide = hall.shape[2]
    half, rows = chips * seqs, groups * seqs
    vocab = lm_ref.shape[1]
    parts, width = pairs.shape[0], pairs.shape[3]
    state_size = b_ref.shape[2]
    links = Links()
    send = links.send
    slot_of = lambda g: (g % 2) * chips + g // 2
    mine = slot_of(group)
    other = {"group": chip * 2 + 1 - core}

    loads = []

    def fetch(src, dst):
        made = pltpu.make_async_copy(src, dst, load.at[len(loads)])
        made.start()
        loads.append(made)
        return made

    own_rows = pl.ds(pl.multiple_of(group * depth, 16), depth)
    have = [fetch(src, dst.at[own_rows]) for src, dst in
            ((z_hbm, z_all), (x_hbm, x_all), (bc_hbm, bc_all), (out_hbm, out_all))]
    have_state = fetch(state_hbm, new_ref)
    have_lm = fetch(lm_hbm, lm_ref)

    hid = hid_ref[...].astype(f32)
    mean_square = jnp.mean(hid * hid, axis=-1, keepdims=True)
    lanes = lax.broadcasted_iota(jnp.int32, (seqs, wide), 1)
    middle = (depth + wide) // 2
    square_halves = halves(mean_square, lanes, depth, middle)
    for p in range(groups):
        hsend[p] = jnp.where(lanes < depth, window(hid, p * depth, depth), square_halves).astype(bf16)
    dt_pad[...] = jnp.zeros_like(dt_pad)
    dt_pad[0:local_heads, 0:depth] = dt_ref[...]

    greet(groups, heads)
    first, dts = [], []
    for j in range(1, groups):
        peer = (group + j) % groups
        first.append(send(hsend.at[peer], hall.at[mine], {"group": peer}, hsem.at[j], hrsem.at[j]))
    dt_rows = dt_all.shape[1]
    for m in range(1, chips):
        dts.append(send(dt_pad.at[pl.ds(0, dt_rows)], dt_all.at[group], {"group": flip(chip, m) * 2 + core},
                        dsem.at[0, m], drsem.at[0, m]))
    dts.append(send(dt_pad.at[pl.ds(0, dt_rows)], dt_all.at[group], other, dsem.at[1, 0], drsem.at[1, 0]))
    piece = depth // PIECES
    units = [(bc_hbm, bc_all, 0, depth)]
    for src, dst in ((z_hbm, z_all), (x_hbm, x_all), (out_hbm, out_all)):
        units += [(src, dst, n * piece, piece) for n in range(PIECES)]
    bulk = Bulk(links, chips, units, bsend, brecv, bpsend, bprecv)

    hall[mine] = hsend[group]
    dt_all[group] = dt_pad[0:dt_rows]
    norm_gain = own_window(norm_in_ref[...][None, :], group, groups, depth)
    final_gain = own_window(fgain_ref[...][None, :], group, groups, depth)
    for made in have[:3]:
        made.wait()
    for made in first:
        made.wait_recv()
    hidden = hall[...].reshape(rows, wide).astype(f32)
    mean_square = hidden[:, depth:depth + 1] + hidden[:, middle:middle + 1]
    normed = (hidden * rms_scale(mean_square) * norm_gain).astype(bf16)[:, :depth]
    at = 0
    for weights in (z_all, x_all, bc_all):
        cols = weights.shape[1]
        made = jnp.dot(normed, weights[own_rows, :], preferred_element_type=f32).astype(bf16)
        ppairs[0, :, at:at + cols], ppairs[1, :, at:at + cols] = made[:half], made[half:]
        at += cols
    made = lax.dot_general(
        normed, dt_pad[:, 0:depth], (((1,), (1,)), ((), ())), preferred_element_type=f32).astype(bf16)
    ppairs[0, :, at:at + 128], ppairs[1, :, at:at + 128] = made[:half], made[half:]
    handed = send(ppairs.at[1 - core], ppair_in, other, qsem, qrsem)
    for m in range(1, chips):
        dts[m - 1].wait_recv()
        view = dt_all.at[flip(chip, m) * 2 + core]
        dts.append(send(view, view, other, dsem.at[1, m], drsem.at[1, m]))
    handed.wait_recv()
    summed = ppairs[core].astype(f32) + ppair_in[...].astype(f32)
    psum[...] = summed.astype(bf16).reshape(psum.shape)
    spread = []
    for m in range(1, chips):
        peer = flip(chip, m)
        spread.append(send(
            psum.at[peer], psum_in.at[m], {"group": peer * 2 + core}, rsem.at[m], rrsem.at[m]))
    psum_in[0] = psum[chip]
    bulk.pump(2)
    for made in spread:
        made.wait_recv()
    branch = jnp.sum(psum_in[...].astype(f32), axis=0).astype(bf16).astype(f32)

    def conv(history, newest, taps, offset):
        total = newest * taps[history.shape[0]:, :]
        for n in range(history.shape[0]):
            total += history[n].astype(f32) * taps[n:n + 1, :]
        return silu(total + offset[None, :])

    gate = branch[:, :inner]
    x_conv = conv(cx_ref[...], branch[:, inner:2 * inner], wx_ref[...], bx_ref[...])
    bc_conv = conv(cbc_ref[...], branch[:, 2 * inner:2 * inner + 2 * state_size], wbc_ref[...], bbc_ref[...])
    raw = branch[:, 2 * inner + 2 * state_size:] + small_ref[0:1, :]
    step = jnp.maximum(raw, 0.0) + jnp.log1p(jnp.exp(-jnp.abs(raw)))
    decay = jnp.exp(-step * jnp.exp(small_ref[1:2, :]))
    place = lax.broadcasted_iota(jnp.int32, (128, inner), 0) * P_SIZE
    lane = lax.broadcasted_iota(jnp.int32, (128, inner), 1)
    chosen = jnp.where((lane >= place) & (lane < place + P_SIZE), 1.0, 0.0)
    by_head = jnp.concatenate([step, jnp.broadcast_to(small_ref[2:3, :], (8, 128))], axis=0)
    by_column = jnp.dot(by_head, chosen, preferred_element_type=f32, precision=lax.Precision.HIGHEST)
    inflow = by_column[:seqs] * x_conv
    skip = by_column[seqs:seqs + 1] * x_conv
    for s in range(seqs):
        inflow_ref[s] = inflow[s:s + 1]
        b_ref[s] = bc_conv[s:s + 1, :state_size]
        c_ref[s] = bc_conv[s:s + 1, state_size:]
        decay_ref[s] = decay[s:s + 1]
    have_state.wait()

    def pair(row):
        high = row.astype(bf16).astype(f32)
        return high, row - high

    def one(s):
        high, low = pair(inflow_ref[s])
        b_high, b_low = pair(b_ref[s])
        place = lax.broadcasted_iota(jnp.int32, (16, inner), 0)
        left = jnp.where(place < 2, high, jnp.where(place < 4, low, 0.0)).astype(bf16)
        place = lax.broadcasted_iota(jnp.int32, (16, state_size), 0)
        right = jnp.where(place % 2 == 0, b_high, b_low).astype(bf16)
        flow = lax.dot_general(left, right, (((0,), (0,)), ((), ())), preferred_element_type=f32)
        decays = decay_ref[s]
        for h in range(local_heads):
            new_ref[s, h] = decays[:, h:h + 1] * new_ref[s, h] + flow[h * P_SIZE:(h + 1) * P_SIZE]
        new = new_ref[s].reshape(inner, state_size).astype(bf16)
        c = jnp.broadcast_to(c_ref[s], (16, state_size)).astype(bf16)
        y = lax.dot_general(c, new, (((1,), (1,)), ((), ())), preferred_element_type=f32)
        y_ref[s] = y[0:1]

    bulk.pump(1)
    for lo, hi in ((0, seqs // 2), (seqs // 2, seqs)):
        pl.loop(lo, hi)(one)
        bulk.pump(1)

    ssm_out = jnp.concatenate([y_ref[s] for s in range(seqs)], axis=0) + skip
    gall[mine] = (ssm_out * silu(gate)).astype(bf16)
    sent = [send(gall.at[mine], gall.at[mine], {"group": flip(chip, m) * 2 + core}, gsem.at[0, m], grsem.at[0, m])
            for m in range(1, chips)]
    near = [send(gall.at[mine], gall.at[mine], other, gsem.at[1, 0], grsem.at[1, 0])]
    bulk.pump(1)
    for m in range(1, chips):
        sent[m - 1].wait_recv()
        view = gall.at[core * chips + flip(chip, m)]
        near.append(send(view, view, other, gsem.at[1, m], grsem.at[1, m]))
    for made in near:
        made.wait_recv()
    have[3].wait()

    gated = gall[...].reshape(rows, inner).astype(f32)
    squares = jnp.sum(gated * gated, axis=-1, keepdims=True)
    scaled = (gated * ngain_ref[...][None, :]).astype(bf16)
    out_rows = out_all[own_rows, :]
    out_rows = jnp.concatenate([out_rows, jnp.zeros((wide - depth, inner), bf16)], axis=0)
    partial = lax.dot_general(scaled, out_rows, (((1,), (1,)), ((), ())), preferred_element_type=f32)
    lanes = lax.broadcasted_iota(jnp.int32, (rows, wide), 1)
    mix[0] = jnp.where(lanes < depth, partial, halves(squares, lanes, depth, middle)).astype(bf16)
    mixes = [
        send(mix.at[0], mix.at[j], {"head": (head + j) % heads}, msend.at[j], mrecv.at[j])
        for j in range(1, heads)
    ]
    bulk.pump(1)
    have_lm.wait()
    for made in mixes:
        made.wait_recv()
    total = jnp.sum(mix[...].astype(f32), axis=0)
    square_total = total[:, depth:depth + 1] + total[:, middle:middle + 1]
    stream = hidden + total * rms_scale(square_total / (inner * heads))
    stream = jnp.where(lanes < depth, stream, 0.0)
    final_squares = jnp.sum(stream * stream, axis=-1, keepdims=True)
    final = (stream * final_gain).astype(bf16)[:, :depth]
    tail_lanes = lax.broadcasted_iota(jnp.int32, (rows, 128), 1)
    packed = halves(jnp.broadcast_to(final_squares, (rows, 128)), tail_lanes, 0, 64).astype(bf16)
    square[0], square[1] = packed[:half], packed[half:]
    pair_sends = [send(square.at[1 - core], square_in, other, psend.at[parts], precv.at[parts])]
    last = []

    def out(source, target, t):
        for m in range(1, chips):
            peer = flip(chip, m)
            last.append(send(
                source.at[peer], target.at[m], {"group": peer * 2 + core}, ssend.at[t, m], srecv.at[t, m]))
        target[0] = source[chip]

    def join(t):
        pair_sends[t + 1].wait_recv()
        joined = pairs[t, core].astype(f32) + pair_in[t].astype(f32)
        sums[t] = joined.astype(bf16).reshape(chips, seqs, width)
        out(sums.at[t], sums_in.at[t], t)

    for t in range(parts):
        block = jnp.dot(
            final, lm_ref[:, t * width:(t + 1) * width], preferred_element_type=f32).astype(bf16)
        pairs[t, 0], pairs[t, 1] = block[:half], block[half:]
        pair_sends.append(send(pairs.at[t, 1 - core], pair_in.at[t], other, psend.at[t], precv.at[t]))
        if t == 0:
            pair_sends[0].wait_recv()
            rest = square[core].astype(f32) + square_in[...].astype(f32)
            rest = rest[:, 0:1] + rest[:, 64:65]
            split = halves(rest, lax.broadcasted_iota(jnp.int32, (half, 128), 1), 0, 64)
            squares_out[...] = split.astype(bf16).reshape(chips, seqs, 128)
            out(squares_out, squares_in, parts)
        else:
            join(t - 1)
    join(parts - 1)
    bulk.pump(2)
    for made in last:
        made.wait_recv()
    bulk.pump(1)

    square_sum = jnp.sum(squares_in[...].astype(f32), axis=0)
    mean_square = (square_sum[:, 0:1] + square_sum[:, 64:65]) / model
    logits = jnp.concatenate([jnp.sum(sums_in[t].astype(f32), axis=0) for t in range(parts)], axis=1)
    logits = logits * rms_scale(mean_square)
    reference = refl_ref[...].astype(f32)
    row = lax.broadcasted_iota(jnp.int32, (seqs, 128), 0)
    tokens = jnp.zeros((seqs, 128), jnp.int32)
    for s in range(seqs):
        tokens = jnp.where(row == s, token_ref[s], tokens)
    columns = lax.broadcasted_iota(jnp.int32, (seqs, vocab), 1) + head * vocab
    picked = jnp.sum(jnp.where(columns == tokens[:, 0:1], logits, 0.0), axis=-1, keepdims=True)
    top = jnp.max(logits, axis=-1, keepdims=True)
    ref_top = jnp.max(reference, axis=-1, keepdims=True)
    weights = jnp.exp(reference - ref_top)
    values = (
        top,
        jnp.sum(jnp.exp(logits - top), axis=-1, keepdims=True),
        ref_top,
        jnp.sum(weights, axis=-1, keepdims=True),
        jnp.sum(weights * (reference - logits), axis=-1, keepdims=True),
        picked,
    )
    slot = lax.broadcasted_iota(jnp.int32, (seqs, 128), 1)
    mine_values = jnp.zeros((seqs, 128), f32)
    for n, value in enumerate(values):
        mine_values = jnp.where(slot == n, value, mine_values)
    stat[0] = mine_values
    stats = [
        send(stat.at[0], stat.at[j], {"head": (head + j) % heads}, tsend.at[j], trecv.at[j])
        for j in range(1, heads)
    ]
    for made in stats:
        made.wait_recv()
    every = stat[...]
    pick = lambda n: every[:, :, n:n + 1]
    top = jnp.max(pick(0), axis=0)
    ref_top = jnp.max(pick(2), axis=0)
    factor = jnp.exp(pick(0) - top[None])
    ref_factor = jnp.exp(pick(2) - ref_top[None])
    roll_sum = jnp.sum(pick(1) * factor, axis=0)
    ref_sum = jnp.sum(pick(3) * ref_factor, axis=0)
    cross = jnp.sum(pick(4) * ref_factor, axis=0)
    picked = jnp.sum(pick(5), axis=0)
    lse_roll = top + jnp.log(roll_sum)
    lse_ref = ref_top + jnp.log(ref_sum)
    result_ref[...] = jnp.where(slot == 0, cross / ref_sum - lse_ref + lse_roll, picked - lse_roll)

    bulk.finish()
    for made in dts[chips - 1:]:
        made.wait_recv()
    links.drain()


def publish_kernel(count, *refs):
    ins, dt_ref, result_ref = refs[:count], refs[count], refs[count + 1]
    outs, dt_out, div_out, prob_out, sems = refs[count + 2:2 * count + 2], *refs[2 * count + 2:]
    made = []
    for n, (src, dst) in enumerate(zip(ins, outs)):
        size = src.shape[0] // 4
        for p in range(4):
            rows = pl.ds(p * size, size)
            made.append(pltpu.make_async_copy(src.at[rows], dst.at[rows], sems.at[n, p]))
            made[-1].start()
    local_heads, model = dt_out.shape
    groups = dt_ref.shape[0]
    depth = model // groups
    dt_out[...] = jnp.concatenate(
        [dt_ref[g].astype(jnp.float32)[:, :depth] for g in range(groups)], axis=1
    )[:local_heads].astype(dt_out.dtype)
    seqs = div_out.shape[1]
    result = result_ref[...]
    same = lax.broadcasted_iota(jnp.int32, (seqs, seqs), 0) == lax.broadcasted_iota(jnp.int32, (seqs, seqs), 1)
    for n, ref in enumerate((div_out, prob_out)):
        ref[...] = jnp.sum(jnp.where(same, result[:, n:n + 1], 0.0), axis=0, keepdims=True)
    for copy in made:
        copy.wait()


def shards(
    groups, heads,
    hidden_in, ssm_state, conv_x_state, conv_bc_state, token_ids, ref_logits,
    in_z, in_x, in_bc, in_dt, out_t, lm_head,
    conv_wx, conv_bx, conv_wbc, conv_bbc, dt_bias, a_log, skip_gain, norm_in, norm_gain, final_gain,
):
    seqs, model = hidden_in.shape
    depth, inner = in_z.shape
    local_heads = a_log.shape[0]
    state_size = ssm_state.shape[3]
    chips = groups // 2
    half, rows = chips * seqs, groups * seqs
    wide = depth + (-depth % 128 or 128)
    vocab = lm_head.shape[0]
    width = vocab // PARTS
    cols = 2 * inner + in_bc.shape[1] + 128
    dt_rows = -(-local_heads // 16) * 16
    small = jnp.pad(jnp.stack([dt_bias, a_log, skip_gain]), ((0, 5), (0, 128 - local_heads)))
    bf16, f32 = jnp.bfloat16, jnp.float32
    vmem, hbm = pl.BlockSpec(memory_space=pltpu.VMEM), pl.BlockSpec(memory_space=pltpu.HBM)
    smem, any_spec = pl.BlockSpec(memory_space=pltpu.SMEM), pl.BlockSpec(memory_space=pl.ANY)
    scratch = pltpu.VMEM
    dma = pltpu.SemaphoreType.DMA
    units = 3 * PIECES + 1
    slots = max(chips, 4)
    gathered = [(groups * depth, w.shape[1]) for w in (in_z, in_x, in_bc, out_t)]
    made = pl.pallas_call(
        functools.partial(step_kernel, groups, heads, local_heads),
        out_shape=[pltpu.VMEM(ssm_state.shape, f32)] + [pltpu.VMEM(shape, bf16) for shape in gathered]
        + [pltpu.VMEM((groups, dt_rows, wide), bf16), pltpu.VMEM((seqs, 128), f32)],
        in_specs=[vmem] * 3 + [smem] + [vmem] * 10 + [hbm] * 6,
        out_specs=[vmem] * 7,
        scratch_shapes=[
            scratch((depth, vocab), bf16),
            scratch((groups, seqs, wide), bf16), scratch((groups, seqs, wide), bf16),
            scratch((2, half, cols), bf16), scratch((half, cols), bf16),
            scratch((chips, seqs, cols), bf16), scratch((chips, seqs, cols), bf16),
            scratch((128, wide), bf16),
            scratch((seqs, 1, inner), f32), scratch((seqs, 1, state_size), f32), scratch((seqs, 1, state_size), f32),
            scratch((seqs, 1, 128), f32), scratch((seqs, 1, inner), f32),
            scratch((groups, seqs, inner), bf16),
            scratch((heads, rows, wide), bf16),
            scratch((PARTS, 2, half, width), bf16), scratch((PARTS, half, width), bf16),
            scratch((PARTS, chips, seqs, width), bf16), scratch((PARTS, chips, seqs, width), bf16),
            scratch((2, half, 128), bf16), scratch((half, 128), bf16),
            scratch((chips, seqs, 128), bf16), scratch((chips, seqs, 128), bf16),
            scratch((heads, seqs, 128), f32),
            dma((6,)), dma((units, slots)), dma((units, slots)), dma((units, slots)), dma((units, slots)),
            dma((groups,)), dma((groups,)), dma((2, chips)), dma((2, chips)), dma, dma,
            dma((chips,)), dma((chips,)), dma((2, chips)), dma((2, chips)),
            dma((heads,)), dma((heads,)), dma((PARTS + 1,)), dma((PARTS + 1,)),
            dma((PARTS + 1, chips)), dma((PARTS + 1, chips)), dma((heads,)), dma((heads,)),
        ],
        compiler_params=pltpu.CompilerParams(
            collective_id=0, has_side_effects=True, vmem_limit_bytes=32 * 1024 * 1024),
        name="step",
    )(
        hidden_in, conv_x_state.transpose(1, 0, 2), conv_bc_state.transpose(1, 0, 2), token_ids, ref_logits, in_dt.T,
        small, conv_wx, conv_bx, conv_wbc, conv_bbc, norm_in, norm_gain, final_gain,
        ssm_state, in_z, in_x, in_bc, out_t, lm_head.T,
    )
    new_state, *rolls, dt_all, result = made
    count = len(rolls) + 1
    published = pl.pallas_call(
        functools.partial(publish_kernel, count),
        out_shape=[jax.ShapeDtypeStruct(ssm_state.shape, f32)] + [jax.ShapeDtypeStruct(v, bf16) for v in gathered]
        + [jax.ShapeDtypeStruct((local_heads, model), bf16)] + [jax.ShapeDtypeStruct((1, seqs), f32)] * 2,
        in_specs=[any_spec] * count + [vmem] * 2,
        out_specs=[any_spec] * count + [vmem] * 3,
        scratch_shapes=[dma((count, 4))],
        compiler_params=pltpu.CompilerParams(vmem_limit_bytes=1 * 1024 * 1024),
        name="publish",
    )(new_state, *rolls, dt_all, result)
    new_state, roll_z, roll_x, roll_bc, roll_out, roll_dt, divergence, logprob = published
    return new_state, divergence[0], logprob[0], roll_z, roll_x, roll_bc, roll_dt.T, roll_out


def solution(mesh):
    return jax.shard_map(
        functools.partial(shards, mesh.shape["group"], mesh.shape["head"]),
        mesh=mesh,
        in_specs=(
            P("group", None),
            P("group", "head", None, None),
            P("group", None, "head"),
            P("group", None, None),
            P("group"),
            P("group", "head"),
            P("group", "head"),
            P("group", "head"),
            P("group", None),
            P("group", "head"),
            P("group", "head"),
            P("head", "group"),
            P(None, "head"),
            P("head"),
            P(),
            P(),
            P("head"),
            P("head"),
            P("head"),
            P(),
            P("head"),
            P(),
        ),
        out_specs=(
            P("group", "head", None, None),
            P("group"),
            P("group"),
            P(None, "head"),
            P(None, "head"),
            P(),
            P(None, "head"),
            P(None, "head"),
        ),
        check_vma=False,
    )
```

time: 180 us -> 134 us (0.74); the launches traced: 177 us -> 134 us
  local copies, waits for them, and re-layouts: 19.8 us -> 0 us
  Pallas kernels: 149 us -> 132 us
  other arithmetic: 7.09 us -> 1.29 us
    pallas_call x4 -> x2, Pallas kernels: 149 us -> 132 us  [the longest x1 121 us: shards(): pl.pallas_call(functools.partial(step_kernel, groups, heads, local_heads)...]
    unnamed x19 -> x0, local copies, waits for them, and re-layouts: 8.98 us -> none
    broadcast_in_dim x5 -> x0, local copies, waits for them, and re-layouts: 4.04 us -> none  [the longest x1 1.33 us: shards(): token_ids[:, None]]
    convert_element_type x2 -> x0, other arithmetic: 3.18 us -> none  [the longest x1 1.61 us: shards(): normed = rms_norm(stream_in, norm_in).astype(jnp.bfloat16)]
    reduce_sum x3 -> x0, other arithmetic: 2.55 us -> none  [the longest x2 1.53 us: causal_conv(): return jax.nn.silu(jnp.sum(window * taps[None, :, :], axis=1) + offset)]
    slice x2 -> x0, local copies, waits for them, and re-layouts: 2.09 us -> none  [the longest x1 1.47 us: shards(): result[:, 1]]
where the time goes in v1:
time: 134 us
  Pallas kernels  132 us (99%)
    pallas_call x1, Pallas kernels, shards(): pl.pallas_call(functools.partial(step_kernel, groups, heads, local_heads)...  121 us
    pallas_call x1, Pallas kernels, shards(): pl.pallas_call(functools.partial(publish_kernel, count), out_shape=[jax.S...  11.1 us

profile of v1, /device:TPU:1, one launch (start us, length us, event | category | flops | bytes accessed | tf_op | source)
XLA Modules:
  0.0 134.1 jit_solution(15753750963607897767)
XLA Ops:
  0.6 1.3 select_maximum_fusion.small_ref
  1.9 121.0 %step.1 = (f32[16,20,64,128]{3,2,1,0:T(8,128)S(1)}, bf16[2560,1280]{1,0:T(8,128)(2,1)S(1)}, bf16[2560,1280]{1,0:T(8,128)(2,1)S(1)}, bf16[2560,256]{1,0:T(8,128)(...) custom-call(bf16[16,2560]{1,0:T(8,128)(2,1)} %hid_ref.1, ...), custom_call_target="tpu_custom_call" | custom-call | tf_op jit(solution)/shard_map/step/pallas_call | solution.py:486
  123.0 11.1 %publish.1 = (f32[16,20,64,128]{3,2,1,0:T(8,128)}, bf16[2560,1280]{1,0:T(8,128)(2,1)}, bf16[2560,1280]{1,0:T(8,128)(2,1)}, bf16[2560,256]{1,0:T(8,128)(2,1)}, bf...) custom-call(f32[16,20,64,128]{3,2,1,0:T(8,128)S(1)} %get-tuple-element.23.refs_0_, ...), custom_call_target="tpu_custom_call" | custom-call | tf_op jit(solution)/shard_map/publish/pallas_call | solution.py:523

commit v2 on v1

--- a/solution.py
+++ b/solution.py
@@ -9,7 +9,7 @@
 
 P_SIZE = 64
 EPSILON = 1e-05
-AHEAD = 2
+AHEAD = 3
 PIECES = 5
 PARTS = 5
 MESH = pl.DeviceIdType.MESH
@@ -57,15 +57,25 @@
         group = lax.axis_index("group")
         self.chip, self.core = group // 2, group % 2
         self.relay = chips == 4
-        self.far, self.near = {}, []
-        self.next = 0
-        for k in range(AHEAD):
-            self.own(k)
-
-    def rows(self, k, chip):
-        src, _, first, count = self.units[k]
-        start = (chip * 2 + self.core) * src.shape[0] + first
-        return self.units[k][1].at[pl.ds(pl.multiple_of(start, 16), count)]
+        self.peers = (1, 2) if self.relay else range(1, chips)
+        self.far, self.near = {}, {}
+        self.next, self.fed = 0, 0
+        self.feed(2)
+
+    def feed(self, ahead):
+        while self.fed < min(self.next + ahead, len(self.units)):
+            self.own(self.fed)
+            self.fed += 1
+
+    def rows(self, k, chip, part=None):
+        src, dst, first, count = self.units[k]
+        if part is not None:
+            count = count // 2
+            first = first + part * count
+        group = chip * 2 + self.core
+        if len(dst.shape) == 3:
+            return dst.at[group, pl.ds(first, count)]
+        return dst.at[pl.ds(pl.multiple_of(group * src.shape[0] + first, 16), count)]
 
     def across(self, k, m, src, dst, slot):
         send, recv = self.sems
@@ -75,47 +85,54 @@
     def hand(self, k, src, dst, slot):
         send, recv = self.pair_sems
         device = {"group": self.chip * 2 + 1 - self.core}
-        self.near.append(self.links.send(src, dst, device, send.at[k, slot], recv.at[k, slot]))
+        self.near.setdefault(k, []).append(self.links.send(src, dst, device, send.at[k, slot], recv.at[k, slot]))
 
     def own(self, k):
         src, _, first, count = self.units[k]
         src, dst = src.at[pl.ds(first, count)], self.rows(k, self.chip)
-        for m in [1, 2] if self.relay else range(1, self.chips):
+        for m in self.peers:
             self.across(k, m, src, dst, m)
         self.hand(k, src, dst, 0)
 
-    def step(self):
+    def step(self, ahead):
         k = self.next
         self.next += 1
-        order = range(1, self.chips)
-        if self.relay:
-            order = (1, 2) if k % 2 == 0 else (2, 1)
-        for m in order:
+        for m in self.peers:
             self.far[k, m].wait_recv()
+            for by, part, slot in self.relays(k):
+                if by == m:
+                    view = self.rows(k, flip(self.chip, m), part)
+                    self.across(k, 3 - m, view, view, slot)
             view = self.rows(k, flip(self.chip, m))
-            if self.relay and m == order[0]:
-                self.across(k, 3 - m, view, view, 3)
             self.hand(k, view, view, m)
-        if k + AHEAD < len(self.units):
-            self.own(k + AHEAD)
+        self.feed(ahead)
         if k:
             self.last(k - 1)
 
+    def relays(self, k):
+        if not self.relay:
+            return []
+        return [(1, 0, 3), (2, 1, 4)] if self.units[k][3] % 32 == 0 else [(1, None, 3)]
+
     def last(self, k):
-        if self.relay:
-            self.far[k, 3].wait_recv()
-            view = self.rows(k, flip(self.chip, 3))
-            self.hand(k, view, view, 3)
-
-    def pump(self, count):
+        for _, part, slot in self.relays(k):
+            self.far[k, slot].wait_recv()
+            view = self.rows(k, flip(self.chip, 3), part)
+            self.hand(k, view, view, slot)
+
+    def pump(self, count, ahead=AHEAD):
         for _ in range(count):
             if self.next < len(self.units):
-                self.step()
+                self.step(ahead)
 
     def finish(self):
         self.pump(len(self.units))
         self.last(len(self.units) - 1)
-        for made in self.near:
+        for k in range(len(self.units)):
+            self.arrive(k)
+
+    def arrive(self, k):
+        for made in self.near.pop(k, []):
             made.wait_recv()
 
 
@@ -148,14 +165,14 @@
 
 def step_kernel(
     groups, heads, local_heads,
-    hid_ref, cx_ref, cbc_ref, token_ref, refl_ref, dt_ref, small_ref,
+    hid_ref, cx_ref, cbc_ref, token_ref, refl_ref, dt_ref, bias_ref, rate_ref, skip_ref,
     wx_ref, bx_ref, wbc_ref, bbc_ref, norm_in_ref, ngain_ref, fgain_ref,
     state_hbm, z_hbm, x_hbm, bc_hbm, out_hbm, lm_hbm,
     new_ref, z_all, x_all, bc_all, out_all, dt_all, result_ref,
-    lm_ref, hsend, hall, ppairs, ppair_in, psum, psum_in, dt_pad, inflow_ref, b_ref, c_ref, decay_ref, y_ref,
+    bc_own, small_ref, lm_ref, hsend, hall, ppairs, ppair_in, psum, psum_in, dt_pad, inflow_ref, b_ref, c_ref, decay_ref, y_ref,
     gall, mix, pairs, pair_in, sums, sums_in, square, square_in, squares_out, squares_in, stat,
     load, bsend, brecv, bpsend, bprecv, hsem, hrsem, dsem, drsem, qsem, qrsem, rsem, rrsem, gsem, grsem,
-    msend, mrecv, psend, precv, ssend, srecv, tsend, trecv,
+    msend, mrecv, psend, precv, ssend, srecv, tsend, trecv, zsem, zrsem, ysem, yrsem,
 ):
     f32, bf16 = jnp.float32, jnp.bfloat16
     chips = groups // 2
@@ -183,8 +200,13 @@
         return made
 
     own_rows = pl.ds(pl.multiple_of(group * depth, 16), depth)
-    have = [fetch(src, dst.at[own_rows]) for src, dst in
-            ((z_hbm, z_all), (x_hbm, x_all), (bc_hbm, bc_all), (out_hbm, out_all))]
+    have = [fetch(src, dst) for src, dst in (
+        (z_hbm, z_all.at[own_rows]), (x_hbm, x_all.at[own_rows]),
+        (bc_hbm, bc_own), (out_hbm, out_all.at[own_rows]))]
+    split = depth % (16 * heads) == 0
+    share_rows = depth // heads if split else depth
+    share_at = pl.multiple_of(head * share_rows, 16) if split else 0
+    have_share = fetch(bc_hbm.at[pl.ds(share_at, share_rows)], bc_all.at[group, pl.ds(share_at, share_rows)])
     have_state = fetch(state_hbm, new_ref)
     have_lm = fetch(lm_hbm, lm_ref)
 
@@ -197,6 +219,9 @@
         hsend[p] = jnp.where(lanes < depth, window(hid, p * depth, depth), square_halves).astype(bf16)
     dt_pad[...] = jnp.zeros_like(dt_pad)
     dt_pad[0:local_heads, 0:depth] = dt_ref[...]
+    small_ref[...] = jnp.zeros_like(small_ref)
+    for n, ref in enumerate((bias_ref, rate_ref, skip_ref)):
+        small_ref[n:n + 1, 0:local_heads] = ref[...][None, :]
 
     greet(groups, heads)
     first, dts = [], []
@@ -209,7 +234,7 @@
                         dsem.at[0, m], drsem.at[0, m]))
     dts.append(send(dt_pad.at[pl.ds(0, dt_rows)], dt_all.at[group], other, dsem.at[1, 0], drsem.at[1, 0]))
     piece = depth // PIECES
-    units = [(bc_hbm, bc_all, 0, depth)]
+    units = [(bc_hbm, bc_all, share_at, share_rows)]
     for src, dst in ((z_hbm, z_all), (x_hbm, x_all), (out_hbm, out_all)):
         units += [(src, dst, n * piece, piece) for n in range(PIECES)]
     bulk = Bulk(links, chips, units, bsend, brecv, bpsend, bprecv)
@@ -226,9 +251,9 @@
     mean_square = hidden[:, depth:depth + 1] + hidden[:, middle:middle + 1]
     normed = (hidden * rms_scale(mean_square) * norm_gain).astype(bf16)[:, :depth]
     at = 0
-    for weights in (z_all, x_all, bc_all):
+    for weights in (z_all[own_rows, :], x_all[own_rows, :], bc_own[...]):
         cols = weights.shape[1]
-        made = jnp.dot(normed, weights[own_rows, :], preferred_element_type=f32).astype(bf16)
+        made = jnp.dot(normed, weights, preferred_element_type=f32).astype(bf16)
         ppairs[0, :, at:at + cols], ppairs[1, :, at:at + cols] = made[:half], made[half:]
         at += cols
     made = lax.dot_general(
@@ -248,7 +273,7 @@
         spread.append(send(
             psum.at[peer], psum_in.at[m], {"group": peer * 2 + core}, rsem.at[m], rrsem.at[m]))
     psum_in[0] = psum[chip]
-    bulk.pump(2)
+    bulk.pump(1)
     for made in spread:
         made.wait_recv()
     branch = jnp.sum(psum_in[...].astype(f32), axis=0).astype(bf16).astype(f32)
@@ -300,9 +325,21 @@
         y_ref[s] = y[0:1]
 
     bulk.pump(1)
-    for lo, hi in ((0, seqs // 2), (seqs // 2, seqs)):
-        pl.loop(lo, hi)(one)
-        bulk.pump(1)
+    passed, crossed = [], []
+    have_share.wait()
+    if split:
+        bulk.arrive(0)
+        for j in range(1, heads):
+            view = bc_all.at[pl.ds(core * chips, chips), pl.ds(share_at, share_rows)]
+            crossed.append(send(view, view, {"head": (head + j) % heads}, zsem.at[j], zrsem.at[j]))
+    for n in range(4):
+        pl.loop(n * seqs // 4, (n + 1) * seqs // 4)(one)
+        bulk.pump(1, 3 if n < 3 else 2)
+    for j, made in enumerate(crossed, 1):
+        made.wait_recv()
+        first_row = pl.multiple_of((head - j + heads) % heads * share_rows, 16)
+        view = bc_all.at[pl.ds(core * chips, chips), pl.ds(first_row, share_rows)]
+        passed.append(send(view, view, other, ysem.at[j], yrsem.at[j]))
 
     ssm_out = jnp.concatenate([y_ref[s] for s in range(seqs)], axis=0) + skip
     gall[mine] = (ssm_out * silu(gate)).astype(bf16)
@@ -330,7 +367,7 @@
         send(mix.at[0], mix.at[j], {"head": (head + j) % heads}, msend.at[j], mrecv.at[j])
         for j in range(1, heads)
     ]
-    bulk.pump(1)
+    bulk.pump(1, 4)
     have_lm.wait()
     for made in mixes:
         made.wait_recv()
@@ -427,6 +464,8 @@
     result_ref[...] = jnp.where(slot == 0, cross / ref_sum - lse_ref + lse_roll, picked - lse_roll)
 
     bulk.finish()
+    for made in passed:
+        made.wait_recv()
     for made in dts[chips - 1:]:
         made.wait_recv()
     links.drain()
@@ -434,7 +473,8 @@
 
 def publish_kernel(count, *refs):
     ins, dt_ref, result_ref = refs[:count], refs[count], refs[count + 1]
-    outs, dt_out, div_out, prob_out, sems = refs[count + 2:2 * count + 2], *refs[2 * count + 2:]
+    outs, smalls, (sems, *held) = refs[count + 2:2 * count + 2], refs[2 * count + 2:2 * count + 5], refs[2 * count + 5:]
+    dt_out, div_out, prob_out = held
     made = []
     for n, (src, dst) in enumerate(zip(ins, outs)):
         size = src.shape[0] // 4
@@ -453,6 +493,9 @@
     same = lax.broadcasted_iota(jnp.int32, (seqs, seqs), 0) == lax.broadcasted_iota(jnp.int32, (seqs, seqs), 1)
     for n, ref in enumerate((div_out, prob_out)):
         ref[...] = jnp.sum(jnp.where(same, result[:, n:n + 1], 0.0), axis=0, keepdims=True)
+    for n, (src, dst) in enumerate(zip(held, smalls)):
+        made.append(pltpu.make_async_copy(src, dst, sems.at[count, n]))
+        made[-1].start()
     for copy in made:
         copy.wait()
 
@@ -474,23 +517,23 @@
     width = vocab // PARTS
     cols = 2 * inner + in_bc.shape[1] + 128
     dt_rows = -(-local_heads // 16) * 16
-    small = jnp.pad(jnp.stack([dt_bias, a_log, skip_gain]), ((0, 5), (0, 128 - local_heads)))
     bf16, f32 = jnp.bfloat16, jnp.float32
     vmem, hbm = pl.BlockSpec(memory_space=pltpu.VMEM), pl.BlockSpec(memory_space=pltpu.HBM)
     smem, any_spec = pl.BlockSpec(memory_space=pltpu.SMEM), pl.BlockSpec(memory_space=pl.ANY)
     scratch = pltpu.VMEM
     dma = pltpu.SemaphoreType.DMA
     units = 3 * PIECES + 1
-    slots = max(chips, 4)
-    gathered = [(groups * depth, w.shape[1]) for w in (in_z, in_x, in_bc, out_t)]
+    slots = max(chips, 5)
+    gathered = [(groups * depth, in_z.shape[1]), (groups * depth, in_x.shape[1]),
+                (groups, depth, in_bc.shape[1]), (groups * depth, out_t.shape[1])]
     made = pl.pallas_call(
         functools.partial(step_kernel, groups, heads, local_heads),
         out_shape=[pltpu.VMEM(ssm_state.shape, f32)] + [pltpu.VMEM(shape, bf16) for shape in gathered]
         + [pltpu.VMEM((groups, dt_rows, wide), bf16), pltpu.VMEM((seqs, 128), f32)],
-        in_specs=[vmem] * 3 + [smem] + [vmem] * 10 + [hbm] * 6,
+        in_specs=[vmem] * 3 + [smem] + [vmem] * 12 + [hbm] * 6,
         out_specs=[vmem] * 7,
         scratch_shapes=[
-            scratch((depth, vocab), bf16),
+            scratch(in_bc.shape, bf16), scratch((8, 128), f32), scratch((depth, vocab), bf16),
             scratch((groups, seqs, wide), bf16), scratch((groups, seqs, wide), bf16),
             scratch((2, half, cols), bf16), scratch((half, cols), bf16),
             scratch((chips, seqs, cols), bf16), scratch((chips, seqs, cols), bf16),
@@ -504,18 +547,19 @@
             scratch((2, half, 128), bf16), scratch((half, 128), bf16),
             scratch((chips, seqs, 128), bf16), scratch((chips, seqs, 128), bf16),
             scratch((heads, seqs, 128), f32),
-            dma((6,)), dma((units, slots)), dma((units, slots)), dma((units, slots)), dma((units, slots)),
+            dma((7,)), dma((units, slots)), dma((units, slots)), dma((units, slots)), dma((units, slots)),
             dma((groups,)), dma((groups,)), dma((2, chips)), dma((2, chips)), dma, dma,
             dma((chips,)), dma((chips,)), dma((2, chips)), dma((2, chips)),
             dma((heads,)), dma((heads,)), dma((PARTS + 1,)), dma((PARTS + 1,)),
             dma((PARTS + 1, chips)), dma((PARTS + 1, chips)), dma((heads,)), dma((heads,)),
+            dma((heads,)), dma((heads,)), dma((heads,)), dma((heads,)),
         ],
         compiler_params=pltpu.CompilerParams(
             collective_id=0, has_side_effects=True, vmem_limit_bytes=32 * 1024 * 1024),
         name="step",
     )(
         hidden_in, conv_x_state.transpose(1, 0, 2), conv_bc_state.transpose(1, 0, 2), token_ids, ref_logits, in_dt.T,
-        small, conv_wx, conv_bx, conv_wbc, conv_bbc, norm_in, norm_gain, final_gain,
+        dt_bias, a_log, skip_gain, conv_wx, conv_bx, conv_wbc, conv_bbc, norm_in, norm_gain, final_gain,
         ssm_state, in_z, in_x, in_bc, out_t, lm_head.T,
     )
     new_state, *rolls, dt_all, result = made
@@ -525,12 +569,13 @@
         out_shape=[jax.ShapeDtypeStruct(ssm_state.shape, f32)] + [jax.ShapeDtypeStruct(v, bf16) for v in gathered]
         + [jax.ShapeDtypeStruct((local_heads, model), bf16)] + [jax.ShapeDtypeStruct((1, seqs), f32)] * 2,
         in_specs=[any_spec] * count + [vmem] * 2,
-        out_specs=[any_spec] * count + [vmem] * 3,
-        scratch_shapes=[dma((count, 4))],
+        out_specs=[any_spec] * (count + 3),
+        scratch_shapes=[dma((count + 1, 4)), scratch((local_heads, model), bf16)] + [scratch((1, seqs), f32)] * 2,
         compiler_params=pltpu.CompilerParams(vmem_limit_bytes=1 * 1024 * 1024),
         name="publish",
     )(new_state, *rolls, dt_all, result)
     new_state, roll_z, roll_x, roll_bc, roll_out, roll_dt, divergence, logprob = published
+    roll_bc = roll_bc.reshape(model, -1)
     return new_state, divergence[0], logprob[0], roll_z, roll_x, roll_bc, roll_dt.T, roll_out
 
 

time: 134 us -> 124 us (0.925)
  Pallas kernels: 132 us -> 123 us
    pallas_call x1, Pallas kernels: 121 us -> 112 us  [shards(): pl.pallas_call(functools.partial(step_kernel, groups, heads, local_heads)...]
where the time goes in v2:
time: 124 us
  Pallas kernels  123 us (99%)
    pallas_call x1, Pallas kernels, shards(): pl.pallas_call(functools.partial(step_kernel, groups, heads, local_heads)...  112 us
    pallas_call x1, Pallas kernels, shards(): pl.pallas_call(functools.partial(publish_kernel, count), out_shape=[jax.S...  10.5 us

profile of v2, /device:TPU:1, one launch (start us, length us, event | category | flops | bytes accessed | tf_op | source)
XLA Modules:
  0.0 123.5 jit_solution(1390790288205292592)
XLA Ops:
  0.6 112.4 %step.1 = (f32[16,20,64,128]{3,2,1,0:T(8,128)S(1)}, bf16[2560,1280]{1,0:T(8,128)(2,1)S(1)}, bf16[2560,1280]{1,0:T(8,128)(2,1)S(1)}, bf16[8,320,256]{2,1,0:T(8,12...) custom-call(bf16[16,2560]{1,0:T(8,128)(2,1)} %hid_ref.1, ...), custom_call_target="tpu_custom_call" | custom-call | tf_op jit(solution)/shard_map/step/pallas_call | solution.py:529
  113.0 10.5 %publish.1 = (f32[16,20,64,128]{3,2,1,0:T(8,128)}, bf16[2560,1280]{1,0:T(8,128)(2,1)}, bf16[2560,1280]{1,0:T(8,128)(2,1)}, bf16[8,320,256]{2,1,0:T(8,128)(2,1)},...) custom-call(f32[16,20,64,128]{3,2,1,0:T(8,128)S(1)} %get-tuple-element.23.refs_0_, ...), custom_call_target="tpu_custom_call" | custom-call | tf_op jit(solution)/shard_map/publish/pallas_call | solution.py:567

commit v3 on v2

--- a/solution.py
+++ b/solution.py
@@ -136,6 +136,49 @@
             made.wait_recv()
 
 
+class Scatter:
+    def __init__(self, links, chips, chip, core, blocks, middle, ends, send_sems, recv_sems):
+        self.blocks, self.middle, self.ends = blocks, middle, ends
+        self.two_phases = chips == 4
+        columns = blocks.shape[2]
+        cut = -(-columns // 256) * 128
+        self.parts = slice(0, cut), slice(cut, columns)
+
+        def send(src, dst, m, slot):
+            device = {"group": flip(chip, m) * 2 + core}
+            return links.send(src, dst, device, send_sems(slot), recv_sems(slot))
+
+        self.send = send
+        if self.two_phases:
+            left, right = (pl.ds(part.start, part.stop - part.start) for part in self.parts)
+            self.sent = [
+                send(blocks.at[pl.ds(1, 2), :, left], middle.at[pl.ds(0, 2), :, left], 1, 0),
+                send(blocks.at[pl.ds(2, 2), :, right], middle.at[pl.ds(0, 2), :, right], 2, 1)]
+        else:
+            self.sent = [send(blocks.at[m], middle.at[m - 1], m, m) for m in range(1, chips)]
+
+    def turn(self):
+        if not self.two_phases:
+            return
+        for n, (block, arrived, m) in enumerate(((3, 1, 2), (1, 0, 1))):
+            self.sent[n].wait_recv()
+            part = self.parts[n]
+            passed = self.blocks[block, :, part].astype(jnp.float32) + self.middle[arrived, :, part].astype(jnp.float32)
+            self.blocks[block, :, part] = passed.astype(jnp.bfloat16)
+            columns = pl.ds(part.start, part.stop - part.start)
+            self.sent.append(self.send(self.blocks.at[block, :, columns], self.ends.at[:, columns], m, 2 + n))
+
+    def total(self):
+        for made in self.sent[2:] if self.two_phases else self.sent:
+            made.wait_recv()
+        f32 = jnp.float32
+        if not self.two_phases:
+            return self.blocks[0].astype(f32) + jnp.sum(self.middle[...].astype(f32), axis=0)
+        return jnp.concatenate(
+            [self.blocks[0, :, part].astype(f32) + self.middle[n, :, part].astype(f32)
+             + self.ends[:, part].astype(f32) for n, part in enumerate(self.parts)], axis=1)
+
+
 def halves(column, lanes, first, split):
     high = column.astype(jnp.bfloat16).astype(jnp.float32)
     return jnp.where(lanes < split, high, column - high)
@@ -169,8 +212,8 @@
     wx_ref, bx_ref, wbc_ref, bbc_ref, norm_in_ref, ngain_ref, fgain_ref,
     state_hbm, z_hbm, x_hbm, bc_hbm, out_hbm, lm_hbm,
     new_ref, z_all, x_all, bc_all, out_all, dt_all, result_ref,
-    bc_own, small_ref, lm_ref, hsend, hall, ppairs, ppair_in, psum, psum_in, dt_pad, inflow_ref, b_ref, c_ref, decay_ref, y_ref,
-    gall, mix, pairs, pair_in, sums, sums_in, square, square_in, squares_out, squares_in, stat,
+    bc_own, small_ref, lm_ref, hsend, hall, ppairs, ppair_in, psum, psum_mid, psum_end, dt_pad, inflow_ref, b_ref, c_ref, decay_ref, y_ref,
+    gall, mix, pairs, pair_in, sums, sums_mid, sums_end, square, square_in, squares_out, squares_in, stat,
     load, bsend, brecv, bpsend, bprecv, hsem, hrsem, dsem, drsem, qsem, qrsem, rsem, rrsem, gsem, grsem,
     msend, mrecv, psend, precv, ssend, srecv, tsend, trecv, zsem, zrsem, ysem, yrsem,
 ):
@@ -187,6 +230,8 @@
     state_size = b_ref.shape[2]
     links = Links()
     send = links.send
+    order = (0, 1, 3, 2) if chips == 4 else tuple(range(chips))
+    chip_rows = [pl.ds(pl.multiple_of(flip(chip, r) * seqs, 16), seqs) for r in order]
     slot_of = lambda g: (g % 2) * chips + g // 2
     mine = slot_of(group)
     other = {"group": chip * 2 + 1 - core}
@@ -265,18 +310,14 @@
         view = dt_all.at[flip(chip, m) * 2 + core]
         dts.append(send(view, view, other, dsem.at[1, m], drsem.at[1, m]))
     handed.wait_recv()
-    summed = ppairs[core].astype(f32) + ppair_in[...].astype(f32)
-    psum[...] = summed.astype(bf16).reshape(psum.shape)
-    spread = []
-    for m in range(1, chips):
-        peer = flip(chip, m)
-        spread.append(send(
-            psum.at[peer], psum_in.at[m], {"group": peer * 2 + core}, rsem.at[m], rrsem.at[m]))
-    psum_in[0] = psum[chip]
+    for n, these in enumerate(chip_rows):
+        psum[n] = (ppairs[core, these, :].astype(f32) + ppair_in[these, :].astype(f32)).astype(bf16)
+    branches = Scatter(
+        links, chips, chip, core, psum, psum_mid, psum_end, lambda k: rsem.at[k], lambda k: rrsem.at[k])
     bulk.pump(1)
-    for made in spread:
-        made.wait_recv()
-    branch = jnp.sum(psum_in[...].astype(f32), axis=0).astype(bf16).astype(f32)
+    branches.turn()
+    bulk.pump(1)
+    branch = branches.total().astype(bf16).astype(f32)
 
     def conv(history, newest, taps, offset):
         total = newest * taps[history.shape[0]:, :]
@@ -381,20 +422,15 @@
     packed = halves(jnp.broadcast_to(final_squares, (rows, 128)), tail_lanes, 0, 64).astype(bf16)
     square[0], square[1] = packed[:half], packed[half:]
     pair_sends = [send(square.at[1 - core], square_in, other, psend.at[parts], precv.at[parts])]
-    last = []
-
-    def out(source, target, t):
-        for m in range(1, chips):
-            peer = flip(chip, m)
-            last.append(send(
-                source.at[peer], target.at[m], {"group": peer * 2 + core}, ssend.at[t, m], srecv.at[t, m]))
-        target[0] = source[chip]
+    last, scatters = [], []
 
     def join(t):
         pair_sends[t + 1].wait_recv()
-        joined = pairs[t, core].astype(f32) + pair_in[t].astype(f32)
-        sums[t] = joined.astype(bf16).reshape(chips, seqs, width)
-        out(sums.at[t], sums_in.at[t], t)
+        for n, these in enumerate(chip_rows):
+            sums[t, n] = (pairs[t, core, these, :].astype(f32) + pair_in[t, these, :].astype(f32)).astype(bf16)
+        scatters.append(Scatter(
+            links, chips, chip, core, sums.at[t], sums_mid.at[t], sums_end.at[t],
+            lambda k: ssend.at[t, k], lambda k: srecv.at[t, k]))
 
     for t in range(parts):
         block = jnp.dot(
@@ -407,18 +443,26 @@
             rest = rest[:, 0:1] + rest[:, 64:65]
             split = halves(rest, lax.broadcasted_iota(jnp.int32, (half, 128), 1), 0, 64)
             squares_out[...] = split.astype(bf16).reshape(chips, seqs, 128)
-            out(squares_out, squares_in, parts)
+            for m in range(1, chips):
+                peer = flip(chip, m)
+                last.append(send(
+                    squares_out.at[peer], squares_in.at[m], {"group": peer * 2 + core},
+                    ssend.at[parts, m], srecv.at[parts, m]))
+            squares_in[0] = squares_out[chip]
         else:
             join(t - 1)
     join(parts - 1)
-    bulk.pump(2)
+    bulk.pump(1)
+    for scatter in scatters:
+        scatter.turn()
+    bulk.pump(1)
     for made in last:
         made.wait_recv()
     bulk.pump(1)
 
     square_sum = jnp.sum(squares_in[...].astype(f32), axis=0)
     mean_square = (square_sum[:, 0:1] + square_sum[:, 64:65]) / model
-    logits = jnp.concatenate([jnp.sum(sums_in[t].astype(f32), axis=0) for t in range(parts)], axis=1)
+    logits = jnp.concatenate([scatter.total() for scatter in scatters], axis=1)
     logits = logits * rms_scale(mean_square)
     reference = refl_ref[...].astype(f32)
     row = lax.broadcasted_iota(jnp.int32, (seqs, 128), 0)
@@ -524,6 +568,7 @@
     dma = pltpu.SemaphoreType.DMA
     units = 3 * PIECES + 1
     slots = max(chips, 5)
+    steps = 2 if chips == 4 else chips - 1
     gathered = [(groups * depth, in_z.shape[1]), (groups * depth, in_x.shape[1]),
                 (groups, depth, in_bc.shape[1]), (groups * depth, out_t.shape[1])]
     made = pl.pallas_call(
@@ -536,14 +581,15 @@
             scratch(in_bc.shape, bf16), scratch((8, 128), f32), scratch((depth, vocab), bf16),
             scratch((groups, seqs, wide), bf16), scratch((groups, seqs, wide), bf16),
             scratch((2, half, cols), bf16), scratch((half, cols), bf16),
-            scratch((chips, seqs, cols), bf16), scratch((chips, seqs, cols), bf16),
+            scratch((chips, seqs, cols), bf16), scratch((steps, seqs, cols), bf16), scratch((seqs, cols), bf16),
             scratch((128, wide), bf16),
             scratch((seqs, 1, inner), f32), scratch((seqs, 1, state_size), f32), scratch((seqs, 1, state_size), f32),
             scratch((seqs, 1, 128), f32), scratch((seqs, 1, inner), f32),
             scratch((groups, seqs, inner), bf16),
             scratch((heads, rows, wide), bf16),
             scratch((PARTS, 2, half, width), bf16), scratch((PARTS, half, width), bf16),
-            scratch((PARTS, chips, seqs, width), bf16), scratch((PARTS, chips, seqs, width), bf16),
+            scratch((PARTS, chips, seqs, width), bf16),
+            scratch((PARTS, steps, seqs, width), bf16), scratch((PARTS, seqs, width), bf16),
             scratch((2, half, 128), bf16), scratch((half, 128), bf16),
             scratch((chips, seqs, 128), bf16), scratch((chips, seqs, 128), bf16),
             scratch((heads, seqs, 128), f32),

time: 124 us -> 120 us (0.968)
  Pallas kernels: 123 us -> 120 us
    pallas_call x1, Pallas kernels: 112 us -> 109 us  [shards(): pl.pallas_call(functools.partial(step_kernel, groups, heads, local_heads)...]
where the time goes in v3:
time: 120 us
  Pallas kernels  120 us (100%)
    pallas_call x1, Pallas kernels, shards(): pl.pallas_call(functools.partial(step_kernel, groups, heads, local_heads)...  109 us
    pallas_call x1, Pallas kernels, shards(): pl.pallas_call(functools.partial(publish_kernel, count), out_shape=[jax.S...  10.5 us

profile of v3, /device:TPU:1, one launch (start us, length us, event | category | flops | bytes accessed | tf_op | source)
XLA Modules:
  0.0 120.3 jit_solution(16341420513084863860)
XLA Ops:
  0.6 109.1 %step.1 = (f32[16,20,64,128]{3,2,1,0:T(8,128)S(1)}, bf16[2560,1280]{1,0:T(8,128)(2,1)S(1)}, bf16[2560,1280]{1,0:T(8,128)(2,1)S(1)}, bf16[8,320,256]{2,1,0:T(8,12...) custom-call(bf16[16,2560]{1,0:T(8,128)(2,1)} %hid_ref.1, ...), custom_call_target="tpu_custom_call" | custom-call | tf_op jit(solution)/shard_map/step/pallas_call | solution.py:574
  109.8 10.5 %publish.1 = (f32[16,20,64,128]{3,2,1,0:T(8,128)}, bf16[2560,1280]{1,0:T(8,128)(2,1)}, bf16[2560,1280]{1,0:T(8,128)(2,1)}, bf16[8,320,256]{2,1,0:T(8,128)(2,1)},...) custom-call(f32[16,20,64,128]{3,2,1,0:T(8,128)S(1)} %get-tuple-element.23.refs_0_, ...), custom_call_target="tpu_custom_call" | custom-call | tf_op jit(solution)/shard_map/publish/pallas_call | solution.py:613
